TPU v7x, 32 devices: a whole 2x2x4 slice. The times are simulated.
32 devices in a mesh: dp: 4 (over x, core), expert: 4 (over z), etp: 2 (over y).
Axes of the slice: x: 2, y: 2, z: 4, core: 2. Of those that a mesh axis runs over, the one named last changes fastest.
Arguments:
- tokens: bfloat16 [4096, 3072], P(('dp', 'expert'), 'etp'), parts along dimension 0, may hold values from -6 to 6
- experts: int32 [4096, 2], P(('dp', 'expert')), parts along dimension 0, may hold values from 0 to 3, all different within a row; in each aligned block of 256 rows (0 to 255, 256 to 511, ...) at most 176 rows name the same one
- mixing: float32 [4096, 2], P(('dp', 'expert')), parts along dimension 0, may hold values from 0.2 to 1
- up_weight: bfloat16 [4, 3072, 8192], P('expert', None, 'etp'), may hold values from -0.109375 to 0.109375
- down_weight: bfloat16 [4, 8192, 3072], P('expert', 'etp'), may hold values from -0.0625 to 0.0625
Outputs:
- mixed: bfloat16 [4096, 3072], P(('dp', 'expert'), 'etp'), parts along dimension 0
There are 4 independent parts, one for each index of `dp`. A program takes and returns all parts, laid end to end along the dimension named above; an argument that names none is the same for every part. Nothing has to cross between parts.
Inputs may be any that keep to these rules, and one draw needn't show every extreme that they name: Each row names two different experts. In the rows of one index of expert (aligned blocks of 256 rows) no expert is named more than 176 times, a bound that some block reaches.
All inputs are finite; a program needn't handle non-finite values.
Results may differ from a plain program's by a relative error of at most 0.0078.
Values may be sent and summed in bfloat16 or wider, within the bound.
A program may use at most 128 MiB of HBM per device.

v0:
```python
import jax
import jax.numpy as jnp
from jax import lax
from jax.sharding import PartitionSpec as P


def slot_table(chosen, expert_count, capacity):
    flat_ids = chosen.reshape(-1)
    one_hot = (flat_ids[:, None] == jnp.arange(expert_count, dtype=jnp.int32)[None, :]).astype(
        jnp.int32
    )
    before = jnp.cumsum(one_hot, axis=0) - one_hot
    position = jnp.sum(before * one_hot, axis=1)
    return (flat_ids * capacity + position).reshape(chosen.shape)


def dispatch_rows(block_tokens, slot_ids, slot_total):
    one_hot = (
        slot_ids[:, :, None] == jnp.arange(slot_total, dtype=jnp.int32)[None, None, :]
    ).astype(jnp.bfloat16)
    placing = jnp.sum(one_hot, axis=1)
    return jnp.einsum(
        "rs,rd->sd", placing, block_tokens, preferred_element_type=jnp.float32
    ).astype(jnp.bfloat16)


def local(tokens, experts, mixing, up_weight, down_weight):
    tok_rows = experts.shape[0]
    part_width = tokens.shape[1]
    expert_count = up_weight.shape[0] * lax.axis_size("expert")
    capacity = 2 * tok_rows // expert_count * 11 // 8
    slot_total = expert_count * capacity
    up_slab = up_weight[0]
    down_slab = down_weight[0]
    slot_ids = slot_table(experts, expert_count, capacity)
    outgoing = dispatch_rows(tokens, slot_ids, slot_total).reshape(
        expert_count, capacity, part_width
    )
    arrived = lax.all_to_all(outgoing, "expert", split_axis=0, concat_axis=0, tiled=True)
    gathered = lax.all_gather(arrived.reshape(slot_total, part_width), "etp", axis=1, tiled=True)
    up_proj = jnp.dot(gathered, up_slab, preferred_element_type=jnp.float32)
    hidden = jax.nn.silu(up_proj).astype(jnp.bfloat16)
    partial_sums = jnp.dot(hidden, down_slab, preferred_element_type=jnp.float32)
    own_cols = lax.psum_scatter(partial_sums, "etp", scatter_dimension=1, tiled=True).astype(
        jnp.bfloat16
    )
    outputs = lax.all_to_all(
        own_cols.reshape(expert_count, capacity, part_width),
        "expert",
        split_axis=0,
        concat_axis=0,
        tiled=True,
    )
    flat_out = outputs.reshape(slot_total, part_width)
    picked = (
        jnp.take(flat_out, slot_ids.reshape(-1), axis=0)
        .reshape(tok_rows, 2, part_width)
        .astype(jnp.float32)
    )
    mixed = jnp.sum(picked * mixing[:, :, None], axis=1)
    return mixed.astype(jnp.bfloat16)


def solution(mesh):
    placed = (
        P(("dp", "expert"), "etp"),
        P(("dp", "expert"), None),
        P(("dp", "expert"), None),
        P("expert", None, "etp"),
        P("expert", "etp", None),
    )
    return jax.shard_map(
        local, mesh=mesh, in_specs=placed, out_specs=P(("dp", "expert"), "etp"), check_vma=False
    )
```

profile of v0, /device:TPU:0, one launch (start us, length us, event | category | flops | bytes accessed | tf_op | source)
XLA Modules:
  0.0 352.5 jit_solution(7086791842899878181)
XLA Ops:
  6.5 0.0 copy-start
  6.5 0.0 all-gather.2.cloned.1.call-start
  6.5 0.9 copy.18
  7.4 0.1 eq.39
  7.6 0.1 reshape.81
  7.7 1.2 reduce-window.6
  9.0 0.2 slice_reduce_fusion
  9.2 0.2 reduce-window.9
  9.4 0.1 add_bitcast_fusion
  9.5 0.1 reduce_sum.35
  9.6 0.1 copy.20
  9.7 0.7 compare_and_fusion
  10.4 0.3 fusion.10
  10.7 0.0 copy-done
  10.7 0.7 convolution_convert_fusion
  11.4 55.9 %all_to_all.10 = bf16[4,176,1536]{2,1,0:T(8,128)(2,1)} all-to-all(bf16[4,176,1536]{2,1,0:T(8,128)(2,1)S(1)} %bitcast.47), channel_id=1, replica_groups=mesh['dp'=4,'expert'=4,'etp'=2] {'expert'}, dimensions={0} | all-to-all | bytes 4325376 | tf_op jit(solution)/shard_map/all_to_all | solution.py:39
  67.3 0.0 all-gather.2.cloned.1.call-update
  67.3 0.0 reduce-scatter.2.cloned.1.call-start
  67.4 57.5 %all-gather.2.cloned.1.call-done = bf16[704,3072]{1,0:T(8,128)(2,1)} async-done(((bf16[704,1536]{1,0:T(8,128)(2,1)}), bf16[704,3072]{1,0:T(8,128)(2,1)}) %all-gather.2.cloned.1.call-update) | async-done | bytes 4325392 | tf_op jit(solution)/shard_map/all_gather | solution.py:40
  124.9 23.9 %multiply_convert_fusion.4 = bf16[704,4096]{1,0:T(8,128)(2,1)S(1)} fusion(bf16[704,3072]{1,0:T(8,128)(2,1)} %all-gather.2.cloned.1.call-done, bf16[1,3072,4096]{2,1,0:T(8,128)(2,1)} %param.8), kind=kOutput, calls=%fused_computation.5.clone.clone.1 | convolution fusion | flops 17731158016 | bytes 35258368 | tf_op jit(solution)/shard_map/dot_general | solution.py:41
  148.8 22.8 %fusion = f32[704,3072]{1,0:T(8,128)} fusion(bf16[1,4096,3072]{2,1,0:T(8,128)(2,1)} %param.9, bf16[704,4096]{1,0:T(8,128)(2,1)S(1)} %multiply_convert_fusion.4), kind=kOutput, calls=%fused_computation.1 | convolution fusion | flops 17716740096 | bytes 39583744 | tf_op jit(solution)/shard_map/dot_general | solution.py:43
  171.6 0.0 reduce-scatter.2.cloned.1.call-update
  171.6 0.0 copy-start.2
  171.6 0.0 copy-start.3
  171.6 102.3 %reduce-scatter.2.cloned.1.call-done = f32[704,1536]{1,0:T(8,128)} async-done(((f32[704,3072]{1,0:T(8,128)}), f32[704,1536]{1,0:T(8,128)}) %reduce-scatter.2.cloned.1.call-update) | async-done | bytes 4325392 | tf_op jit(solution)/shard_map/reduce_scatter | solution.py:44
  273.9 3.8 %convert_element_type.32 = bf16[704,1536]{1,0:T(8,128)(2,1)} convert(f32[704,1536]{1,0:T(8,128)} %reduce-scatter.2.cloned.1.call-done) | non-fusion elementwise | flops 1081344 | bytes 6488064 | tf_op jit(solution)/shard_map/convert_element_type | solution.py:44
  277.7 4.6 %all-to-all-start.1 = ((bf16[4,176,1536]{2,1,0:T(8,128)(2,1)}), bf16[4,176,1536]{2,1,0:T(8,128)(2,1)S(1)}, u32[]{:S(2)}, u32[]{:S(2)}) async-start(bf16[4,176,1536]{2,1,0:T(8,128)(2,1)} %bitcast.48), calls=%async_computation.2 | async-start | bytes 4325376 | tf_op jit(solution)/shard_map/all_to_all | solution.py:47
  282.4 0.0 copy-done.2
  282.4 0.1 copy.22
  282.5 0.1 mul.40
  282.7 0.2 copy.21
  282.8 0.0 copy-done.3
  282.9 0.1 copy.23
  283.0 48.8 %all-to-all-done.1 = bf16[4,176,1536]{2,1,0:T(8,128)(2,1)S(1)} async-done(((bf16[4,176,1536]{2,1,0:T(8,128)(2,1)}), bf16[4,176,1536]{2,1,0:T(8,128)(2,1)S(1)}, u32[]{:S(2)}, u32[]{:S(2)}) %all-to-all-start.1) | async-done | bytes 2162720 | tf_op jit(solution)/shard_map/all_to_all | solution.py:47
  331.8 0.0 copy-start.1
  331.8 2.9 gather_fusion
  334.8 3.5 gather.7
  338.3 7.4 %multiply_reduce_fusion = bf16[256,1536]{1,0:T(8,128)(2,1)} fusion(bf16[256,2,1536]{2,1,0:T(2,128)(2,1)S(1)} %gather.7, pred[256,2]{1,0:T(8,128)(4,1)S(1)} %copy.21, f32[256,2]{1,0:T(8,128)S(1)} %copy.23), kind=kLoop, calls=%fused_computation.8 | loop fusion | flops 2752512 | bytes 2361856 | tf_op jit(solution)/shard_map/reduce_sum | solution.py:60
  345.7 0.0 copy-done.1
  (5 shorter events, 0.0 us)
Async XLA Ops:
  6.5 4.2 %copy-start = (bf16[256,1536]{1,0:T(8,128)(2,1)S(1)}, bf16[256,1536]{1,0:T(8,128)(2,1)}, u32[]{:S(2)}) copy-start(bf16[256,1536]{1,0:T(8,128)(2,1)} %param.5) | copy-start | bytes 2359300
  6.5 118.4 %all-gather.2.cloned.1.call-start = ((), (), s32[]{:S(2)}) async-start(), calls=%async_computation.3 | async-start | bytes 6488064 | tf_op jit(solution)/shard_map/all_gather | solution.py:40
  67.3 206.6 %reduce-scatter.2.cloned.1.call-start = ((), (), s32[]{:S(2)}) async-start(), calls=%async_computation.4 | async-start | bytes 12976128 | tf_op jit(solution)/shard_map/reduce_scatter | solution.py:44
  171.6 110.7 %copy-start.2 = (s32[256,2]{0,1:T(2,128)S(1)}, s32[256,2]{0,1:T(2,128)}, u32[]{:S(2)}) copy-start(s32[256,2]{0,1:T(2,128)} %param.6) | copy-start | bytes 6148
  171.6 111.2 %copy-start.3 = (f32[256,2]{0,1:T(2,128)S(1)}, f32[256,2]{0,1:T(2,128)}, u32[]{:S(2)}) copy-start(f32[256,2]{0,1:T(2,128)} %param.7) | copy-start | bytes 6148
  277.7 54.1 %all-to-all-start.1 = ((bf16[4,176,1536]{2,1,0:T(8,128)(2,1)}), bf16[4,176,1536]{2,1,0:T(8,128)(2,1)S(1)}, u32[]{:S(2)}, u32[]{:S(2)}) async-start(bf16[4,176,1536]{2,1,0:T(8,128)(2,1)} %bitcast.48), calls=%async_computation.2 | async-start | bytes 4325376 | tf_op jit(solution)/shard_map/all_to_all | solution.py:47
  331.8 13.9 %copy-start.1 = (bf16[256,1536]{1,0:T(8,128)(2,1)S(1)}, bf16[256,1536]{1,0:T(8,128)(2,1)}, u32[]{:S(2)}) copy-start(bf16[256,1536]{1,0:T(8,128)(2,1)} %param.5) | copy-start | bytes 2359300
Sparse Core Ops, SparseCore 0:
  67.4 57.4 all-gather.1
  171.7 102.1 reduce-scatter.1
where the time goes:
time: 353 us
  waiting for transfers between devices  209 us (59%)
  blocking collectives  55.9 us (16%)
  matrix products  47.4 us (13%)
  other arithmetic  13.8 us (4%)
  between operations  13.5 us (4%)
  local copies, waits for them, and re-layouts  8.65 us (2%)
  starting transfers between devices  4.67 us (1%)
    reduce_scatter x1, waiting for transfers between devices, local(): lax.psum_scatter(partial_sums, 'etp', scatter_dimension=1, tiled=True)  102 us
    all_gather x1, waiting for transfers between devices, local(): lax.all_gather(arrived.reshape(slot_total, part_width), 'etp', axis=1, ti...  57.5 us
    all_to_all x1, blocking collectives, local(): lax.all_to_all(outgoing, 'expert', split_axis=0, concat_axis=0, tiled=True)  55.9 us
    all_to_all x1, waiting for transfers between devices, local(): lax.all_to_all(own_cols.reshape(expert_count, capacity, part_width), 'exp...  48.8 us
    dot_general x1, matrix products, local(): up_proj = jnp.dot(gathered, up_slab, preferred_element_type=jnp.float32)  23.9 us
    dot_general x1, matrix products, local(): jnp.dot(hidden, down_slab, preferred_element_type=jnp.float32)  22.8 us
    reduce_sum x1, other arithmetic, local(): mixed = jnp.sum(picked * mixing[:, :, None], axis=1)  7.44 us
  transfers between devices with their start and end apart: 3, of which 3 were waited for; matrix products, arithmetic and copies ran while one was open for 0% of the time, Pallas kernels for 0%

commit v1 on v0

v1 whole, which is shorter than its diff:
```python
import functools

import jax
import jax.numpy as jnp
from jax import lax
from jax.experimental import pallas as pl
from jax.experimental.pallas import tpu as pltpu
from jax.sharding import PartitionSpec as P

MESH = pl.DeviceIdType.MESH


def flipped(index, shift, count):
    total, bit = 0, 1
    while bit < count:
        digit = lax.rem(lax.div(index, bit), 2)
        total = total + (1 - digit if shift & bit else digit) * bit
        bit *= 2
    return total


def layer_kernel(
    chunks, sharers, tile,
    tok_ref, up_ref, down_ref, out_ref,
    up_v, down_v, full, hidden, other, own, landed,
    up_sem, down_sem, local_sem,
    zs_sem, zr_sem, ys_sem, yr_sem, bs_sem, br_sem, os_sem, or_sem,
):
    width = tok_ref.shape[2]
    units = up_v.shape[1]
    my_z = lax.axis_index("expert")
    my_y = lax.axis_index("etp")
    z_peer = [{"expert": flipped(my_z, s, chunks)} for s in range(chunks)]
    y_index = [flipped(my_y, t, sharers) for t in range(sharers)]
    y_peer = [{"etp": y_index[t]} for t in range(sharers)]

    def remote(src, dst, send, recv, peer):
        return pltpu.make_async_remote_copy(
            src_ref=src, dst_ref=dst, send_sem=send, recv_sem=recv,
            device_id=peer, device_id_type=MESH,
        )

    def columns(t):
        return pl.ds(t * width, width)

    up_copy, down_copy = [], []
    for t in range(sharers):
        begin = pl.multiple_of(y_index[t] * width, 128)
        up_copy.append(
            pltpu.make_async_copy(
                up_ref.at[pl.ds(begin, width), :], up_v.at[columns(t), :], up_sem.at[t]
            )
        )
        down_copy.append(
            pltpu.make_async_copy(
                down_ref.at[:, pl.ds(begin, width)], down_v.at[:, columns(t)], down_sem.at[t]
            )
        )
    first = pltpu.make_async_copy(tok_ref.at[0], full.at[0, :, columns(0)], local_sem.at[0])

    barrier = pltpu.get_barrier_semaphore()
    for peer in z_peer[1:] + y_peer[1:]:
        pl.semaphore_signal(barrier, inc=1, device_id=peer, device_id_type=MESH)
    pl.semaphore_wait(barrier, chunks - 1 + sharers - 1)

    z_go = [None] + [
        remote(
            tok_ref.at[s], full.at[s, :, columns(0)], zs_sem.at[s], zr_sem.at[s], z_peer[s]
        )
        for s in range(1, chunks)
    ]
    y_go = [
        [
            remote(
                full.at[s, :, columns(0)] if s else tok_ref.at[0],
                full.at[s, :, columns(t)], ys_sem.at[s, t], yr_sem.at[s, t], y_peer[t],
            )
            for t in range(1, sharers)
        ]
        for s in range(chunks)
    ]
    y_back = [
        [
            remote(
                other.at[s, t - 1], landed.at[s, t - 1], bs_sem.at[s, t], br_sem.at[s, t],
                y_peer[t],
            )
            for t in range(1, sharers)
        ]
        for s in range(chunks)
    ]
    z_back = [None] + [
        remote(own.at[s], out_ref.at[s], os_sem.at[s], or_sem.at[s], z_peer[s])
        for s in range(1, chunks)
    ]
    last = pltpu.make_async_copy(own.at[0], out_ref.at[0], local_sem.at[1])

    for copy in y_go[0]:
        copy.start()
    for s in range(1, chunks):
        z_go[s].start()
    first.start()
    for copy in up_copy + down_copy:
        copy.start()

    def forward(s):
        z_go[s].wait_recv()
        for copy in y_go[s]:
            copy.start()

    def up(s):
        @pl.loop(0, units // tile)
        def _(i):
            at = pl.ds(pl.multiple_of(i * tile, tile), tile)
            value = jnp.dot(full[s], up_v[:, at], preferred_element_type=jnp.float32)
            hidden[:, at] = (value / (1.0 + jnp.exp(-value))).astype(jnp.bfloat16)

    def down(s, t):
        target = other.at[s, t - 1] if t else own.at[s]

        @pl.loop(0, width // tile)
        def _(i):
            at = pl.multiple_of(i * tile, tile)
            value = jnp.dot(
                hidden[...], down_v[:, pl.ds(t * width + at, tile)],
                preferred_element_type=jnp.float32,
            )
            target[:, pl.ds(at, tile)] = value.astype(jnp.bfloat16)

    def start_back(s):
        for copy in y_back[s]:
            copy.start()

    def finish(s):
        for copy in y_back[s]:
            copy.wait_recv()
        total = own[s].astype(jnp.float32)
        for t in range(1, sharers):
            total = total + landed[s, t - 1].astype(jnp.float32)
        own[s] = total.astype(jnp.bfloat16)
        (z_back[s] if s else last).start()

    half = chunks // 2
    forward(1)
    first.wait()
    for s in range(chunks):
        if s >= 2 and s + 1 < chunks:
            forward(s + 1)
        for copy in y_go[s]:
            copy.wait_recv()
        if s == 0:
            for copy in up_copy:
                copy.wait()
        up(s)
        if s == 1 and chunks > 2:
            forward(2)
        if s == 0:
            for copy in down_copy:
                copy.wait()
        for t in range(1, sharers):
            down(s, t)
        if s == 0 or s >= half:
            start_back(s)
        down(s, 0)
    for s in range(1, half):
        start_back(s)
    for s in list(range(half, chunks)) + list(range(half)):
        finish(s)

    last.wait()
    for s in range(chunks):
        for copy in y_go[s] + y_back[s]:
            copy.wait_send()
        if s:
            z_go[s].wait_send()
            z_back[s].wait_send()
            z_back[s].wait_recv()


def run_layer(outgoing, up_slab, down_slab, sharers):
    chunks, capacity, width = outgoing.shape
    model, units = up_slab.shape
    tile = 512 if width % 512 == 0 else 256
    bf16 = jnp.bfloat16
    dma = pltpu.SemaphoreType.DMA
    anywhere = pl.BlockSpec(memory_space=pl.ANY)
    return pl.pallas_call(
        functools.partial(layer_kernel, chunks, sharers, tile),
        out_shape=jax.ShapeDtypeStruct(outgoing.shape, bf16),
        in_specs=[anywhere] * 3,
        out_specs=anywhere,
        scratch_shapes=[
            pltpu.VMEM((model, units), bf16),
            pltpu.VMEM((units, model), bf16),
            pltpu.VMEM((chunks, capacity, model), bf16),
            pltpu.VMEM((capacity, units), bf16),
            pltpu.VMEM((chunks, sharers - 1, capacity, width), bf16),
            pltpu.VMEM((chunks, capacity, width), bf16),
            pltpu.VMEM((chunks, sharers - 1, capacity, width), bf16),
            dma((sharers,)), dma((sharers,)), dma((2,)),
            dma((chunks,)), dma((chunks,)),
            dma((chunks, sharers)), dma((chunks, sharers)),
            dma((chunks, sharers)), dma((chunks, sharers)),
            dma((chunks,)), dma((chunks,)),
        ],
        compiler_params=pltpu.CompilerParams(
            collective_id=0, has_side_effects=True, vmem_limit_bytes=67_043_328
        ),
    )(outgoing, up_slab, down_slab)


def slot_table(chosen, expert_count, capacity):
    flat_ids = chosen.reshape(-1)
    one_hot = (flat_ids[:, None] == jnp.arange(expert_count, dtype=jnp.int32)[None, :]).astype(
        jnp.int32
    )
    before = jnp.cumsum(one_hot, axis=0) - one_hot
    position = jnp.sum(before * one_hot, axis=1)
    return (flat_ids * capacity + position).reshape(chosen.shape)


def local(tokens, experts, mixing, up_weight, down_weight):
    tok_rows = experts.shape[0]
    part_width = tokens.shape[1]
    sharers = lax.axis_size("etp")
    expert_count = up_weight.shape[0] * lax.axis_size("expert")
    capacity = 2 * tok_rows // expert_count * 11 // 8
    slot_total = expert_count * capacity
    relative = experts ^ lax.axis_index("expert")
    slot_ids = slot_table(relative, expert_count, capacity)
    slots = jnp.arange(slot_total, dtype=jnp.int32)
    hits = slot_ids[:, :, None] == slots[None, None, :]
    placing = jnp.sum(hits.astype(jnp.bfloat16), axis=1)
    outgoing = jnp.einsum(
        "rs,rd->sd", placing, tokens, preferred_element_type=jnp.float32
    ).astype(jnp.bfloat16)
    outputs = run_layer(
        outgoing.reshape(expert_count, capacity, part_width), up_weight[0], down_weight[0], sharers
    ).reshape(slot_total, part_width)
    weights = jnp.sum(jnp.where(hits, mixing[:, :, None], 0.0), axis=1)
    coarse = weights.astype(jnp.bfloat16)
    fine = (weights - coarse.astype(jnp.float32)).astype(jnp.bfloat16)
    mixed = jnp.dot(coarse, outputs, preferred_element_type=jnp.float32) + jnp.dot(
        fine, outputs, preferred_element_type=jnp.float32
    )
    return mixed.astype(jnp.bfloat16)


def solution(mesh):
    placed = (
        P(("dp", "expert"), "etp"),
        P(("dp", "expert"), None),
        P(("dp", "expert"), None),
        P("expert", None, "etp"),
        P("expert", "etp", None),
    )
    return jax.shard_map(
        local, mesh=mesh, in_specs=placed, out_specs=P(("dp", "expert"), "etp"), check_vma=False
    )
```

time: 353 us -> 138 us (0.39)
  waiting for transfers between devices: 209 us -> 0 us
  Pallas kernels: 0 us -> 126 us
  blocking collectives: 55.9 us -> 0 us
  matrix products: 47.4 us -> 6.53 us
  between operations: 13.5 us -> 0.1 us
  other arithmetic: 13.8 us -> 3.74 us
  local copies, waits for them, and re-layouts: 8.65 us -> 1.6 us
  starting transfers between devices: 4.67 us -> 0 us
    pallas_call x0 -> x1, Pallas kernels: none -> 126 us  [run_layer(): pl.pallas_call(functools.partial(layer_kernel, chunks, sharers, tile), ou...]
    reduce_scatter x1 -> x0, waiting for transfers between devices: 102 us -> none  [local(): lax.psum_scatter(partial_sums, 'etp', scatter_dimension=1, tiled=True)]
    all_gather x1 -> x0, waiting for transfers between devices: 57.5 us -> none  [local(): lax.all_gather(arrived.reshape(slot_total, part_width), 'etp', axis=1, ti...]
    all_to_all x1 -> x0, blocking collectives: 55.9 us -> none  [local(): lax.all_to_all(outgoing, 'expert', split_axis=0, concat_axis=0, tiled=True)]
    all_to_all x1 -> x0, waiting for transfers between devices: 48.8 us -> none  [local(): lax.all_to_all(own_cols.reshape(expert_count, capacity, part_width), 'exp...]
    dot_general x3, matrix products: 47.4 us -> 6.53 us  [the longest x1 2.77 us: local(): jnp.dot(coarse, outputs, preferred_element_type=jnp.float32)]
    gather x2 -> x0, local copies, waits for them, and re-layouts: 6.45 us -> none  [local(): jnp.take(flat_out, slot_ids.reshape(-1), axis=0)]
    reduce_sum x2, other arithmetic: 7.73 us -> 2.2 us  [the longest x1 1.89 us: local(): weights = jnp.sum(jnp.where(hits, mixing[:, :, None], 0.0), axis=1)]
  transfers between devices with their start and end apart: 3 -> 0, of which waited for: 3 -> 0; matrix products, arithmetic and copies ran while one was open for 0% -> 0% of each run, Pallas kernels for 0% -> 0%
where the time goes in v1:
time: 138 us
  Pallas kernels  126 us (91%)
  matrix products  6.53 us (5%)
  other arithmetic  3.74 us (3%)
  local copies, waits for them, and re-layouts  1.6 us (1%)
    pallas_call x1, Pallas kernels, run_layer(): pl.pallas_call(functools.partial(layer_kernel, chunks, sharers, tile), ou...  126 us
    dot_general x1, matrix products, local(): jnp.dot(coarse, outputs, preferred_element_type=jnp.float32)  2.77 us

profile of v1, /device:TPU:0, one launch (start us, length us, event | category | flops | bytes accessed | tf_op | source)
XLA Modules:
  0.0 137.8 jit_solution(15048817197381698138)
XLA Ops:
  0.0 0.0 copy-start.2
  0.0 0.9 copy.10
  0.9 0.1 eq.38
  1.1 0.1 eq.42
  1.2 1.2 reduce-window.6
  2.4 0.2 slice_reduce_fusion
  2.7 0.2 reduce-window.9
  2.8 0.1 add_bitcast_fusion
  2.9 0.1 reduce_sum.33
  3.1 0.1 copy.11
  3.2 0.3 fusion.2
  3.5 1.9 %select_reduce_fusion = f32[256,704]{0,1:T(8,128)} fusion(f32[256,2]{0,1:T(2,128)} %param.7, s32[256,2]{0,1:T(2,128)S(1)} %copy.11), kind=kLoop, calls=%fused_computation.3 | loop fusion | flops 901120 | bytes 724992 | tf_op jit(solution)/shard_map/reduce_sum | solution.py:240
  5.4 0.0 copy-done.2
  5.4 2.1 %convolution_convert_fusion = bf16[704,1536]{1,0:T(8,128)(2,1)} fusion(bf16[256,704]{0,1:T(8,128)(2,1)S(1)} %fusion.2, bf16[256,1536]{1,0:T(8,128)(2,1)S(1)} %copy-done.2), kind=kOutput, calls=%fused_computation | convolution fusion | flops 554729472 | bytes 3309568 | tf_op jit(solution)/shard_map/rs,rd->sd/dot_general | solution.py:234
  7.5 125.8 %shard_map.55 = bf16[4,176,1536]{2,1,0:T(8,128)(2,1)} custom-call(bf16[4,176,1536]{2,1,0:T(8,128)(2,1)} %bitcast.31, bf16[3072,4096]{1,0:T(8,128)(2,1)} %bitcast.27, bf16[4096,3072]{1,0:T(8,128)(2,1)} %bitcast.28), custom_call_target="tpu_custom_call" | custom-call | tf_op jit(solution)/shard_map/pallas_call | solution.py:187
  133.3 0.0 copy-start
  133.3 0.0 copy-start.1
  133.3 2.8 %fusion.4 = f32[256,1536]{1,0:T(8,128)S(1)} fusion(bf16[704,1536]{1,0:T(8,128)(2,1)} %bitcast.29, f32[256,704]{0,1:T(8,128)} %select_reduce_fusion), kind=kOutput, calls=%fused_computation.9 | convolution fusion | flops 553828352 | bytes 4456448 | tf_op jit(solution)/shard_map/dot_general | solution.py:243
  136.1 0.0 copy-done
  136.1 0.0 copy-done.1
  136.1 1.7 %fusion = bf16[256,1536]{1,0:T(8,128)(2,1)} fusion(f32[256,1536]{1,0:T(8,128)S(1)} %fusion.4, bf16[704,1536]{1,0:T(8,128)(2,1)S(1)} %bitcast.30, f32[256,704]{0,1:T(8,128)S(1)} %copy-done.1), kind=kOutput, calls=%fused_computation.2 | convolution fusion | flops 555155456 | bytes 5242880 | tf_op jit(solution)/shard_map/dot_general | solution.py:243
  (4 shorter events, 0.1 us)
Async XLA Ops:
  0.0 5.4 %copy-start.2 = (bf16[256,1536]{1,0:T(8,128)(2,1)S(1)}, bf16[256,1536]{1,0:T(8,128)(2,1)}, u32[]{:S(2)}) copy-start(bf16[256,1536]{1,0:T(8,128)(2,1)} %param.5) | copy-start | bytes 2359300
  133.3 2.8 %copy-start = (bf16[4,176,1536]{2,1,0:T(8,128)(2,1)S(1)}, bf16[4,176,1536]{2,1,0:T(8,128)(2,1)}, u32[]{:S(2)}) copy-start(bf16[4,176,1536]{2,1,0:T(8,128)(2,1)} %shard_map.55) | copy-start | bytes 6488068
  133.3 2.8 %copy-start.1 = (f32[256,704]{0,1:T(8,128)S(1)}, f32[256,704]{0,1:T(8,128)}, u32[]{:S(2)}) copy-start(f32[256,704]{0,1:T(8,128)} %select_reduce_fusion) | copy-start | bytes 2162692

commit v2 on v1

v2 whole, which is shorter than its diff:
```python
import functools

import jax
import jax.numpy as jnp
from jax import lax
from jax.experimental import pallas as pl
from jax.experimental.pallas import tpu as pltpu
from jax.sharding import PartitionSpec as P

MESH = pl.DeviceIdType.MESH


def flipped(index, shift, count):
    total, bit = 0, 1
    while bit < count:
        digit = lax.rem(lax.div(index, bit), 2)
        total = total + (1 - digit if shift & bit else digit) * bit
        bit *= 2
    return total


def layer_kernel(
    chunks, sharers, tile,
    tok_ref, experts_ref, mixing_ref, up_ref, down_ref, out_ref, share_ref,
    up_v, down_v, full, hidden, other, own, landed, share_v,
    up_sem, down_sem, local_sem,
    zs_sem, zr_sem, ys_sem, yr_sem, bs_sem, br_sem, os_sem, or_sem,
):
    rows, width = tok_ref.shape
    capacity = full.shape[1]
    units = up_v.shape[1]
    my_z = lax.axis_index("expert")
    my_y = lax.axis_index("etp")
    z_index = [flipped(my_z, s, chunks) for s in range(chunks)]
    z_peer = [{"expert": z_index[s]} for s in range(chunks)]
    y_index = [flipped(my_y, t, sharers) for t in range(sharers)]
    y_peer = [{"etp": y_index[t]} for t in range(sharers)]
    cut = -(-capacity // 32) * 16
    pieces = [pl.ds(0, cut), pl.ds(cut, capacity - cut)]
    both = range(len(pieces))

    def remote(src, dst, send, recv, peer):
        return pltpu.make_async_remote_copy(
            src_ref=src, dst_ref=dst, send_sem=send, recv_sem=recv,
            device_id=peer, device_id_type=MESH,
        )

    def columns(t):
        return pl.ds(t * width, width)

    up_copy, down_copy = [], []
    for t in range(sharers):
        begin = pl.multiple_of(y_index[t] * width, 128)
        up_copy.append(
            pltpu.make_async_copy(
                up_ref.at[pl.ds(begin, width), :], up_v.at[columns(t), :], up_sem.at[t]
            )
        )
        down_copy.append(
            pltpu.make_async_copy(
                down_ref.at[:, pl.ds(begin, width)], down_v.at[:, columns(t)], down_sem.at[t]
            )
        )
    for copy in up_copy + down_copy:
        copy.start()

    barrier = pltpu.get_barrier_semaphore()
    for peer in z_peer[1:] + y_peer[1:]:
        pl.semaphore_signal(barrier, inc=1, device_id=peer, device_id_type=MESH)

    z_go = [None] + [
        [
            remote(
                own.at[s, piece], full.at[s, piece, columns(0)],
                zs_sem.at[s, p], zr_sem.at[s, p], z_peer[s],
            )
            for p, piece in enumerate(pieces)
        ]
        for s in range(1, chunks)
    ]
    y_go = [
        [
            [
                remote(
                    full.at[s, piece, columns(0)], full.at[s, piece, columns(t)],
                    ys_sem.at[s, t, p], yr_sem.at[s, t, p], y_peer[t],
                )
                for t in range(1, sharers)
            ]
            for p, piece in enumerate(pieces)
        ]
        for s in range(chunks)
    ]
    y_back = [
        [
            [
                remote(
                    other.at[s, t - 1, piece], landed.at[s, t - 1, piece],
                    bs_sem.at[s, t, p], br_sem.at[s, t, p], y_peer[t],
                )
                for t in range(1, sharers)
            ]
            for p, piece in enumerate(pieces)
        ]
        for s in range(chunks)
    ]
    z_back = [
        pltpu.make_async_copy(own.at[0, piece], out_ref.at[0, piece], local_sem.at[p])
        for p, piece in enumerate(pieces)
    ]
    z_back = [z_back] + [
        [
            remote(
                own.at[s, piece], out_ref.at[s, piece], os_sem.at[s, p], or_sem.at[s, p],
                z_peer[s],
            )
            for p, piece in enumerate(pieces)
        ]
        for s in range(1, chunks)
    ]
    share_copy = pltpu.make_async_copy(share_v, share_ref, local_sem.at[len(pieces)])

    lanes = lax.broadcasted_iota(jnp.int32, (rows, 128), 1)
    named = [experts_ref[:, k : k + 1] for k in range(2)]
    hot = [jnp.where(lanes == named[k], 1.0, 0.0) for k in range(2)]
    above = jnp.where(
        lax.broadcasted_iota(jnp.int32, (rows, rows), 0)
        > lax.broadcasted_iota(jnp.int32, (rows, rows), 1),
        1.0, 0.0,
    ).astype(jnp.bfloat16)
    counts = [
        jnp.dot(above, hot[k].astype(jnp.bfloat16), preferred_element_type=jnp.float32)
        for k in range(2)
    ]
    counts[1] = counts[1] + jnp.sum(hot[0], axis=0, keepdims=True)
    place = [jnp.sum(counts[k] * hot[k], axis=1, keepdims=True) for k in range(2)]

    def dispatch(s):
        slots = lax.broadcasted_iota(jnp.int32, (rows, capacity), 1).astype(jnp.float32)
        hit = jnp.zeros((rows, capacity), jnp.float32)
        for k in range(2):
            mine = jnp.where(named[k] == z_index[s], place[k], -1.0)
            hit = hit + jnp.where(slots == mine, 1.0, 0.0)
        chunk = lax.dot_general(
            hit.astype(jnp.bfloat16), tok_ref[...], (((0,), (0,)), ((), ())),
            preferred_element_type=jnp.float32,
        ).astype(jnp.bfloat16)
        if s:
            own[s] = chunk
        else:
            full[0, :, columns(0)] = chunk

    def forward(s, p):
        z_go[s][p].wait_recv()
        for copy in y_go[s][p]:
            copy.start()

    def up(s):
        @pl.loop(0, units // tile)
        def _(i):
            at = pl.ds(pl.multiple_of(i * tile, tile), tile)
            value = jnp.dot(full[s], up_v[:, at], preferred_element_type=jnp.float32)
            hidden[:, at] = (value / (1.0 + jnp.exp(-value))).astype(jnp.bfloat16)

    def down(s, t):
        target = other.at[s, t - 1] if t else own.at[s]

        @pl.loop(0, width // tile)
        def _(i):
            at = pl.multiple_of(i * tile, tile)
            value = jnp.dot(
                hidden[...], down_v[:, pl.ds(t * width + at, tile)],
                preferred_element_type=jnp.float32,
            )
            target[:, pl.ds(at, tile)] = value.astype(jnp.bfloat16)

    def start_back(s):
        for p in both:
            for copy in y_back[s][p]:
                copy.start()

    def finish(s, p):
        for copy in y_back[s][p]:
            copy.wait_recv()
        total = own[s, pieces[p]].astype(jnp.float32)
        for t in range(1, sharers):
            total = total + landed[s, t - 1, pieces[p]].astype(jnp.float32)
        own[s, pieces[p]] = total.astype(jnp.bfloat16)
        z_back[s][p].start()

    half = chunks // 2
    order = [0, half] + list(range(1, half)) + list(range(half + 1, chunks))
    dispatch(half)
    pl.semaphore_wait(barrier, chunks - 1 + sharers - 1)
    for copy in z_go[half]:
        copy.start()
    for s in [0] + order[2:]:
        dispatch(s)
        for p in both:
            for copy in [z_go[s][p]] if s else y_go[0][p]:
                copy.start()

    slots = lax.broadcasted_iota(jnp.int32, share_v.shape, 1).astype(jnp.float32)
    share = jnp.zeros(share_v.shape, jnp.float32)
    for k in range(2):
        slot = place[k]
        for s in range(1, chunks):
            slot = slot + jnp.where(named[k] == z_index[s], 1.0 * s * capacity, 0.0)
        share = share + jnp.where(slots == slot, mixing_ref[:, k : k + 1], 0.0)
    share_v[...] = share.astype(jnp.bfloat16)
    share_copy.start()

    forward(half, 0)
    for i, s in enumerate(order):
        for p in both:
            for copy in y_go[s][p]:
                copy.wait_recv()
        if i == 0:
            for copy in up_copy:
                copy.wait()
        up(s)
        if i == 0:
            forward(half, 1)
            for copy in down_copy:
                copy.wait()
        elif i + 2 < chunks:
            forward(order[i + 2], 0)
        for t in range(1, sharers):
            down(s, t)
        if s >= half:
            start_back(s)
        if i == chunks - 1:
            for done in order[:-1]:
                if done >= half:
                    for p in both:
                        finish(done, p)
        if s:
            for copy in z_go[s]:
                copy.wait_send()
        down(s, 0)
        if i + 2 < chunks:
            for p in both[1 if i else 0 :]:
                forward(order[i + 2], p)
    rest = list(range(1, half)) + [0]
    for s in rest:
        start_back(s)
    for s in order[-1:] + rest:
        for p in both:
            finish(s, p)

    share_copy.wait()
    for s in range(chunks):
        for p in both:
            for copy in y_go[s][p] + y_back[s][p]:
                copy.wait_send()
            if s:
                z_back[s][p].wait_send()
                z_back[s][p].wait_recv()
            else:
                z_back[s][p].wait()


def run_layer(tokens, experts, mixing, up_slab, down_slab, chunks, capacity, sharers):
    rows, width = tokens.shape
    model, units = up_slab.shape
    tile = 512 if width % 512 == 0 else 256
    bf16 = jnp.bfloat16
    dma = pltpu.SemaphoreType.DMA
    anywhere = pl.BlockSpec(memory_space=pl.ANY)
    near = pl.BlockSpec(memory_space=pltpu.VMEM)
    return pl.pallas_call(
        functools.partial(layer_kernel, chunks, sharers, tile),
        out_shape=(
            jax.ShapeDtypeStruct((chunks, capacity, width), bf16),
            jax.ShapeDtypeStruct((rows, chunks * capacity), bf16),
        ),
        in_specs=[near] * 3 + [anywhere] * 2,
        out_specs=(anywhere, anywhere),
        scratch_shapes=[
            pltpu.VMEM((model, units), bf16),
            pltpu.VMEM((units, model), bf16),
            pltpu.VMEM((chunks, capacity, model), bf16),
            pltpu.VMEM((capacity, units), bf16),
            pltpu.VMEM((chunks, sharers - 1, capacity, width), bf16),
            pltpu.VMEM((chunks, capacity, width), bf16),
            pltpu.VMEM((chunks, sharers - 1, capacity, width), bf16),
            pltpu.VMEM((rows, chunks * capacity), bf16),
            dma((sharers,)), dma((sharers,)), dma((3,)),
            dma((chunks, 2)), dma((chunks, 2)),
            dma((chunks, sharers, 2)), dma((chunks, sharers, 2)),
            dma((chunks, sharers, 2)), dma((chunks, sharers, 2)),
            dma((chunks, 2)), dma((chunks, 2)),
        ],
        compiler_params=pltpu.CompilerParams(
            collective_id=0, has_side_effects=True, vmem_limit_bytes=67_043_328
        ),
    )(tokens, experts, mixing, up_slab, down_slab)


def local(tokens, experts, mixing, up_weight, down_weight):
    tok_rows, part_width = tokens.shape
    sharers = lax.axis_size("etp")
    expert_count = up_weight.shape[0] * lax.axis_size("expert")
    capacity = 2 * tok_rows // expert_count * 11 // 8
    outputs, share = run_layer(
        tokens, experts, mixing, up_weight[0], down_weight[0], expert_count, capacity, sharers
    )
    outputs = outputs.reshape(expert_count * capacity, part_width)
    return jnp.dot(share, outputs, preferred_element_type=jnp.float32).astype(jnp.bfloat16)


def solution(mesh):
    placed = (
        P(("dp", "expert"), "etp"),
        P(("dp", "expert"), None),
        P(("dp", "expert"), None),
        P("expert", None, "etp"),
        P("expert", "etp", None),
    )
    return jax.shard_map(
        local, mesh=mesh, in_specs=placed, out_specs=P(("dp", "expert"), "etp"), check_vma=False
    )
```

time: 138 us -> 136 us (0.986)
  other arithmetic: 3.74 us -> 0 us
  matrix products: 6.53 us -> 3.41 us
  Pallas kernels: 126 us -> 129 us
    pallas_call x1, Pallas kernels: 126 us -> 129 us  [run_layer(): pl.pallas_call(functools.partial(layer_kernel, chunks, sharers, tile), ou...]
    dot_general x3 -> x1, matrix products: 6.53 us -> 3.41 us  [local(): jnp.dot(share, outputs, preferred_element_type=jnp.float32)]
    reduce_sum x3 -> x0, other arithmetic: 2.22 us -> none  [the longest x1 1.89 us: local(): weights = jnp.sum(jnp.where(hits, mixing[:, :, None], 0.0), axis=1)]
    unnamed x7 -> x2, local copies, waits for them, and re-layouts: 0.9 us -> 2.94 us
    another operation x2 -> x0, other arithmetic: 1.41 us -> none
where the time goes in v2:
time: 136 us
  Pallas kernels  129 us (95%)
  matrix products  3.41 us (3%)
  local copies, waits for them, and re-layouts  2.94 us (2%)
    pallas_call x1, Pallas kernels, run_layer(): pl.pallas_call(functools.partial(layer_kernel, chunks, sharers, tile), ou...  129 us
    dot_general x1, matrix products, local(): jnp.dot(share, outputs, preferred_element_type=jnp.float32)  3.41 us
    unnamed x2, local copies, waits for them, and re-layouts  2.94 us

profile of v2, /device:TPU:0, one launch (start us, length us, event | category | flops | bytes accessed | tf_op | source)
XLA Modules:
  0.0 135.5 jit_solution(17948402580583260661)
XLA Ops:
  0.0 1.5 %copy.6.experts_ref = s32[256,2]{1,0:T(8,128)} copy(s32[256,2]{0,1:T(2,128)} %param.6) | data formatting | bytes 4096 | tf_op args[1]
  1.5 1.5 %copy.7.mixing_ref = f32[256,2]{1,0:T(8,128)} copy(f32[256,2]{0,1:T(2,128)} %param.7) | data formatting | bytes 4096 | tf_op args[2]
  2.9 129.2 %shard_map.55 = (bf16[4,176,1536]{2,1,0:T(8,128)(2,1)}, bf16[256,704]{1,0:T(8,128)(2,1)}) custom-call(bf16[256,1536]{1,0:T(8,128)(2,1)} %tok_ref.1, s32[256,2]{1,0:T(8,128)} %copy.6.experts_ref, f32[256,2]{1,0:T(8,128)} %copy.7.mixing_ref, bf16[3072,4096]{1,0:T(8,128)(2,1)} %bitcast.5, bf16[4096,3072]{1,0:T(8,128)(2,1)} %bitcast.6), custom_call_target="tpu_custom_call" | custom-call | tf_op jit(solution)/shard_map/pallas_call | solution.py:271
  132.1 3.4 %convolution_convert_fusion = bf16[256,1536]{1,0:T(8,128)(2,1)} fusion(bf16[256,704]{1,0:T(8,128)(2,1)} %get-tuple-element.7, bf16[704,1536]{1,0:T(8,128)(2,1)} %bitcast.7), kind=kOutput, calls=%fused_computation | convolution fusion | flops 554041344 | bytes 3309568 | tf_op jit(solution)/shard_map/dot_general | solution.py:309

commit v3 on v2

--- a/solution.py
+++ b/solution.py
@@ -21,7 +21,7 @@
 
 def layer_kernel(
     chunks, sharers, tile,
-    tok_ref, experts_ref, mixing_ref, up_ref, down_ref, out_ref, share_ref,
+    tok_ref, routes_ref, up_ref, down_ref, out_ref, share_ref,
     up_v, down_v, full, hidden, other, own, landed, share_v,
     up_sem, down_sem, local_sem,
     zs_sem, zr_sem, ys_sem, yr_sem, bs_sem, br_sem, os_sem, or_sem,
@@ -120,8 +120,11 @@
     ]
     share_copy = pltpu.make_async_copy(share_v, share_ref, local_sem.at[len(pieces)])
 
-    lanes = lax.broadcasted_iota(jnp.int32, (rows, 128), 1)
-    named = [experts_ref[:, k : k + 1] for k in range(2)]
+    lanes = lax.broadcasted_iota(jnp.int32, (rows, 128), 1).astype(jnp.float32)
+    routes = jnp.transpose(routes_ref[...])
+    named = [routes[:, k : k + 1] for k in range(2)]
+    mixing = [routes[:, k : k + 1] for k in range(2, 4)]
+    z_name = [z_index[s].astype(jnp.float32) for s in range(chunks)]
     hot = [jnp.where(lanes == named[k], 1.0, 0.0) for k in range(2)]
     above = jnp.where(
         lax.broadcasted_iota(jnp.int32, (rows, rows), 0)
@@ -139,7 +142,7 @@
         slots = lax.broadcasted_iota(jnp.int32, (rows, capacity), 1).astype(jnp.float32)
         hit = jnp.zeros((rows, capacity), jnp.float32)
         for k in range(2):
-            mine = jnp.where(named[k] == z_index[s], place[k], -1.0)
+            mine = jnp.where(named[k] == z_name[s], place[k], -1.0)
             hit = hit + jnp.where(slots == mine, 1.0, 0.0)
         chunk = lax.dot_general(
             hit.astype(jnp.bfloat16), tok_ref[...], (((0,), (0,)), ((), ())),
@@ -189,10 +192,10 @@
         z_back[s][p].start()
 
     half = chunks // 2
-    order = [0, half] + list(range(1, half)) + list(range(half + 1, chunks))
-    dispatch(half)
+    order = list(range(chunks))
+    dispatch(order[1])
     pl.semaphore_wait(barrier, chunks - 1 + sharers - 1)
-    for copy in z_go[half]:
+    for copy in z_go[order[1]]:
         copy.start()
     for s in [0] + order[2:]:
         dispatch(s)
@@ -205,12 +208,12 @@
     for k in range(2):
         slot = place[k]
         for s in range(1, chunks):
-            slot = slot + jnp.where(named[k] == z_index[s], 1.0 * s * capacity, 0.0)
-        share = share + jnp.where(slots == slot, mixing_ref[:, k : k + 1], 0.0)
+            slot = slot + jnp.where(named[k] == z_name[s], 1.0 * s * capacity, 0.0)
+        share = share + jnp.where(slots == slot, mixing[k], 0.0)
     share_v[...] = share.astype(jnp.bfloat16)
     share_copy.start()
 
-    forward(half, 0)
+    forward(order[1], 0)
     for i, s in enumerate(order):
         for p in both:
             for copy in y_go[s][p]:
@@ -220,7 +223,7 @@
                 copy.wait()
         up(s)
         if i == 0:
-            forward(half, 1)
+            forward(order[1], 1)
             for copy in down_copy:
                 copy.wait()
         elif i + 2 < chunks:
@@ -260,7 +263,7 @@
                 z_back[s][p].wait()
 
 
-def run_layer(tokens, experts, mixing, up_slab, down_slab, chunks, capacity, sharers):
+def run_layer(tokens, routes, up_slab, down_slab, chunks, capacity, sharers):
     rows, width = tokens.shape
     model, units = up_slab.shape
     tile = 512 if width % 512 == 0 else 256
@@ -274,7 +277,7 @@
             jax.ShapeDtypeStruct((chunks, capacity, width), bf16),
             jax.ShapeDtypeStruct((rows, chunks * capacity), bf16),
         ),
-        in_specs=[near] * 3 + [anywhere] * 2,
+        in_specs=[near] * 2 + [anywhere] * 2,
         out_specs=(anywhere, anywhere),
         scratch_shapes=[
             pltpu.VMEM((model, units), bf16),
@@ -294,7 +297,7 @@
         compiler_params=pltpu.CompilerParams(
             collective_id=0, has_side_effects=True, vmem_limit_bytes=67_043_328
         ),
-    )(tokens, experts, mixing, up_slab, down_slab)
+    )(tokens, routes, up_slab, down_slab)
 
 
 def local(tokens, experts, mixing, up_weight, down_weight):
@@ -302,8 +305,11 @@
     sharers = lax.axis_size("etp")
     expert_count = up_weight.shape[0] * lax.axis_size("expert")
     capacity = 2 * tok_rows // expert_count * 11 // 8
+    routes = jnp.concatenate(
+        [experts.T.astype(jnp.float32), mixing.T, jnp.zeros((4, tok_rows), jnp.float32)]
+    )
     outputs, share = run_layer(
-        tokens, experts, mixing, up_weight[0], down_weight[0], expert_count, capacity, sharers
+        tokens, routes, up_weight[0], down_weight[0], expert_count, capacity, sharers
     )
     outputs = outputs.reshape(expert_count * capacity, part_width)
     return jnp.dot(share, outputs, preferred_element_type=jnp.float32).astype(jnp.bfloat16)

time: 136 us -> 125 us (0.919)
  Pallas kernels: 129 us -> 119 us
  local copies, waits for them, and re-layouts: 2.94 us -> 0.08 us
  other arithmetic: 0 us -> 2.03 us
    pallas_call x1, Pallas kernels: 129 us -> 119 us  [run_layer(): pl.pallas_call(functools.partial(layer_kernel, chunks, sharers, tile), ou...]
    unnamed x2 -> x0, local copies, waits for them, and re-layouts: 2.94 us -> none
where the time goes in v3:
time: 125 us
  Pallas kernels  119 us (95%)
  matrix products  3.41 us (3%)
  other arithmetic  2.03 us (2%)
    pallas_call x1, Pallas kernels, run_layer(): pl.pallas_call(functools.partial(layer_kernel, chunks, sharers, tile), ou...  119 us
    dot_general x1, matrix products, local(): jnp.dot(share, outputs, preferred_element_type=jnp.float32)  3.41 us

profile of v3, /device:TPU:0, one launch (start us, length us, event | category | flops | bytes accessed | tf_op | source)
XLA Modules:
  0.0 124.6 jit_solution(2754720694309155319)
XLA Ops:
  0.0 0.1 pad.2.clone
  0.1 0.7 convert_bitcast_fusion
  0.8 1.3 %maximum_maximum_fusion.routes_ref = f32[8,256]{1,0:T(8,128)} fusion(f32[2,256]{1,0:T(2,128)} %bitcast.10, f32[2,256]{1,0:T(2,128)S(1)} %convert_bitcast_fusion, f32[8]{0:T(128)S(1)} %pad.2.clone), kind=kLoop, calls=%fused_computation.1 | loop fusion | flops 4096 | bytes 12320 | tf_op jit(solution)/shard_map/concatenate | solution.py:308
  2.1 119.1 %shard_map.55 = (bf16[4,176,1536]{2,1,0:T(8,128)(2,1)}, bf16[256,704]{1,0:T(8,128)(2,1)}) custom-call(bf16[256,1536]{1,0:T(8,128)(2,1)} %tok_ref.1, f32[8,256]{1,0:T(8,128)} %maximum_maximum_fusion.routes_ref, bf16[3072,4096]{1,0:T(8,128)(2,1)} %bitcast.8, bf16[4096,3072]{1,0:T(8,128)(2,1)} %bitcast.9), custom_call_target="tpu_custom_call" | custom-call | tf_op jit(solution)/shard_map/pallas_call | solution.py:274
  121.2 3.4 %convolution_convert_fusion = bf16[256,1536]{1,0:T(8,128)(2,1)} fusion(bf16[256,704]{1,0:T(8,128)(2,1)} %get-tuple-element.7, bf16[704,1536]{1,0:T(8,128)(2,1)} %bitcast.11), kind=kOutput, calls=%fused_computation | convolution fusion | flops 554041344 | bytes 3309568 | tf_op jit(solution)/shard_map/dot_general | solution.py:315
  (1 shorter events, 0.0 us)
